TPU v7x, 8 devices: a whole 2x2x1 slice. The times are simulated.
8 devices in a mesh: rep: 2 (over y, z), dp: 4 (over x, core).
Axes of the slice: x: 2, y: 2, z: 1, core: 2. Of those that a mesh axis runs over, the one named last changes fastest.
Arguments:
- a: bfloat16 [8, 4, 4096, 768], P(('rep', 'dp')), parts along dimension 0
- g: bfloat16 [8, 4, 4096, 3072], P(('rep', 'dp')), parts along dimension 0
Outputs:
- output: bfloat16 [8, 768, 3072], P('rep'), parts along dimension 0
There are 2 independent parts. A program takes and returns all parts, laid end to end along the dimension named above; each array names one.
All inputs are finite; a program needn't handle non-finite values.
Results may differ from a plain program's by a relative error of at most 0.012.
Values are sent between devices in bfloat16 or wider.
A program may use at most 2 GiB of HBM per device.

v0:
```python
import jax
import jax.numpy as jnp


def solution(mesh):
    groups = mesh.shape["rep"]

    def step(a, g):
        a, g = (t.reshape(groups, -1, *t.shape[1:]) for t in (a, g))
        sums = jnp.einsum("rsntd,rsntf->rndf", a, g, preferred_element_type=jnp.float32)
        return sums.astype(jnp.bfloat16).reshape(-1, *sums.shape[2:])

    return step
```

profile of v0, /device:TPU:0, one launch (start us, length us, event | category | flops | bytes accessed | tf_op | source)
XLA Modules:
  0.0 729.6 jit_solution(15959505667501455865)
XLA Ops:
  0.0 88.8 %fusion.3 = f32[1,4,768,3072]{3,2,1,0:T(8,128)} fusion(bf16[1,4,4096,3072]{3,2,1,0:T(8,128)(2,1)} %param.1, bf16[1,4,4096,768]{3,2,1,0:T(8,128)(2,1)} %param), kind=kOutput, calls=%fused_computation.4 | convolution fusion | flops 77309411328 | bytes 163577856 | tf_op jit(solution)/rsntd,rsntf->rndf/dot_general | solution.py:10
  88.8 640.8 %all-reduce.2 = bf16[1,4,768,3072]{3,2,1,0:T(8,128)(2,1)} all-reduce(f32[1,4,768,3072]{3,2,1,0:T(8,128)} %fusion.3), channel_id=1, replica_groups=[2,4]<=[8], use_global_device_ids=true, to_apply=%add.clone | all-reduce | flops 9437184 | bytes 56623104 | tf_op jit(solution)/rsntd,rsntf->rndf/dot_general | solution.py:10
where the time goes:
time: 730 us
  blocking collectives  641 us (88%)
  matrix products  88.8 us (12%)
    dot_general x1, blocking collectives, step(): jnp.einsum('rsntd,rsntf->rndf', a, g, preferred_element_type=jnp.float32)  641 us
    dot_general x1, matrix products, step(): jnp.einsum('rsntd,rsntf->rndf', a, g, preferred_element_type=jnp.float32)  88.8 us

commit v1 on v0

v1 whole, which is shorter than its diff:
```python
import functools

import jax
import jax.numpy as jnp
from jax import lax
from jax.experimental import pallas as pl
from jax.experimental.pallas import tpu as pltpu
from jax.sharding import PartitionSpec as P

MESH = pl.DeviceIdType.MESH
WIDTH = 256
G_SLOTS = 3


def kernel(a_hbm, g_hbm, out, a_buf, a_t, g_buf, own, stage, came,
           a_sem, g_sem, d_send, d_recv, x_send, x_recv, f_send, f_recv):
    mats, tokens, rows = a_hbm.shape
    cols = g_hbm.shape[2]
    half = rows // 2
    tiles = cols // WIDTH
    steps = mats * tiles

    rep = lax.axis_index("rep")
    me = lax.axis_index("dp")
    core = lax.rem(me, 2)
    partner = me + 1 - 2 * core
    across = lax.rem(me + 2, 4)
    mine = pl.ds(pl.multiple_of(core * half, half), half)
    theirs = pl.ds(pl.multiple_of((1 - core) * half, half), half)

    def a_copy(n):
        return pltpu.make_async_copy(a_hbm.at[n], a_buf, a_sem)

    def g_copy(n, t, slot):
        return pltpu.make_async_copy(
            g_hbm.at[n, :, pl.ds(pl.multiple_of(t * WIDTH, WIDTH), WIDTH)],
            g_buf.at[slot], g_sem.at[slot])

    def block(n, t):
        return out.at[n, mine, pl.ds(pl.multiple_of(t * WIDTH, WIDTH), WIDTH)]

    def block_theirs(n, t):
        return out.at[n, theirs, pl.ds(pl.multiple_of(t * WIDTH, WIDTH), WIDTH)]

    def d_copy(n, t, i):
        return pltpu.make_async_remote_copy(
            stage.at[lax.rem(i, 2)], block_theirs(n, t), d_send.at[lax.rem(i, 2)], d_recv.at[i],
            device_id=(rep, partner), device_id_type=MESH)

    def d_arrival(n, t, i):
        return pltpu.make_async_remote_copy(
            stage.at[lax.rem(i, 2)], block(n, t), d_send.at[lax.rem(i, 2)], d_recv.at[i],
            device_id=(rep, partner), device_id_type=MESH)

    def x_copy(n, t, i):
        return pltpu.make_async_remote_copy(
            block(n, t), came.at[i], x_send.at[i], x_recv.at[i],
            device_id=(rep, across), device_id_type=MESH)

    def f_copy(n, t, i):
        return pltpu.make_async_remote_copy(
            block(n, t), block(n, t), f_send.at[i], f_recv.at[i],
            device_id=(rep, partner), device_id_type=MESH)

    def f_arrival(n, t, i):
        return pltpu.make_async_remote_copy(
            block_theirs(n, t), block_theirs(n, t), f_send.at[i], f_recv.at[i],
            device_id=(rep, partner), device_id_type=MESH)

    a_copy(0).start()
    for s in range(G_SLOTS - 1):
        g_copy(0, s, s).start()

    barrier = pltpu.get_barrier_semaphore()
    for other in (partner, across):
        pl.semaphore_signal(barrier, 1, device_id=(rep, other), device_id_type=MESH)
    pl.semaphore_wait(barrier, 2)

    @pl.loop(0, mats)
    def _(n):
        a_copy(n).wait()

        @pl.loop(0, tokens // 256)
        def _(k):
            at = pl.ds(pl.multiple_of(k * 256, 256), 256)
            a_t[:, at] = a_buf[at, :].T

        @pl.when(n + 1 < mats)
        def _():
            a_copy(n + 1).start()

        @pl.loop(0, tiles)
        def _(t):
            i = n * tiles + t
            slot = lax.rem(i, G_SLOTS)
            ahead = i + G_SLOTS - 1

            @pl.when(ahead < steps)
            def _():
                g_copy(ahead // tiles, lax.rem(ahead, tiles), lax.rem(ahead, G_SLOTS)).start()

            g_copy(n, t, slot).wait()

            @pl.when(i >= 2)
            def _():
                before = i - 2
                d_copy(before // tiles, lax.rem(before, tiles), before).wait_send()

            stage[lax.rem(i, 2)] = jnp.dot(
                a_t[theirs, :], g_buf[slot], preferred_element_type=jnp.float32
            ).astype(jnp.bfloat16)
            d_copy(n, t, i).start()
            own[...] = jnp.dot(a_t[mine, :], g_buf[slot], preferred_element_type=jnp.float32)
            d_arrival(n, t, i).wait_recv()
            b = block(n, t)
            b[...] = (own[...] + b[...].astype(jnp.float32)).astype(jnp.bfloat16)
            x_copy(n, t, i).start()

    for i in (steps - 2, steps - 1):
        d_copy(i // tiles, i % tiles, i).wait_send()

    @pl.loop(0, steps)
    def _(i):
        n, t = i // tiles, lax.rem(i, tiles)
        c = x_copy(n, t, i)
        c.wait_send()
        c.wait_recv()
        b = block(n, t)
        b[...] = (b[...].astype(jnp.float32) + came[i].astype(jnp.float32)).astype(jnp.bfloat16)
        f_copy(n, t, i).start()

    @pl.loop(0, steps)
    def _(i):
        n, t = i // tiles, lax.rem(i, tiles)
        f_copy(n, t, i).wait_send()
        f_arrival(n, t, i).wait_recv()


def solution(mesh):
    def step(a, g):
        a, g = a[0], g[0]
        mats, tokens, rows = a.shape
        cols = g.shape[2]
        half = rows // 2
        steps = mats * (cols // WIDTH)
        dma = pltpu.SemaphoreType.DMA
        return pl.pallas_call(
            kernel,
            out_shape=pltpu.VMEM((mats, rows, cols), jnp.bfloat16),
            in_specs=[pl.BlockSpec(memory_space=pl.ANY)] * 2,
            out_specs=pl.BlockSpec(memory_space=pltpu.VMEM),
            scratch_shapes=[
                pltpu.VMEM((tokens, rows), jnp.bfloat16),
                pltpu.VMEM((rows, tokens), jnp.bfloat16),
                pltpu.VMEM((G_SLOTS, tokens, WIDTH), jnp.bfloat16),
                pltpu.VMEM((half, WIDTH), jnp.float32),
                pltpu.VMEM((2, half, WIDTH), jnp.bfloat16),
                pltpu.VMEM((steps, half, WIDTH), jnp.bfloat16),
                dma, dma((G_SLOTS,)), dma((2,)), dma((steps,)),
                dma((steps,)), dma((steps,)), dma((steps,)), dma((steps,)),
            ],
            compiler_params=pltpu.CompilerParams(
                collective_id=0, has_side_effects=True, vmem_limit_bytes=42 << 20),
            name="sums",
        )(a, g)

    return jax.shard_map(
        step, mesh=mesh, in_specs=(P(("rep", "dp")), P(("rep", "dp"))), out_specs=P("rep"),
        check_vma=False)
```

time: 730 us -> 226 us (0.31)
  blocking collectives: 641 us -> 0 us
  Pallas kernels: 0 us -> 219 us
  matrix products: 88.8 us -> 0 us
    dot_general x1 -> x0, blocking collectives: 641 us -> none  [step(): jnp.einsum('rsntd,rsntf->rndf', a, g, preferred_element_type=jnp.float32)]
    pallas_call x0 -> x1, Pallas kernels: none -> 219 us  [step(): pl.pallas_call(kernel, out_shape=pltpu.VMEM((mats, rows, cols), jnp.bfloa...]
    dot_general x1 -> x0, matrix products: 88.8 us -> none  [step(): jnp.einsum('rsntd,rsntf->rndf', a, g, preferred_element_type=jnp.float32)]
where the time goes in v1:
time: 226 us
  Pallas kernels  219 us (97%)
  local copies, waits for them, and re-layouts  6.85 us (3%)
    pallas_call x1, Pallas kernels, step(): pl.pallas_call(kernel, out_shape=pltpu.VMEM((mats, rows, cols), jnp.bfloa...  219 us
    unnamed x1, local copies, waits for them, and re-layouts  6.85 us

profile of v1, /device:TPU:0, one launch (start us, length us, event | category | flops | bytes accessed | tf_op | source)
XLA Modules:
  0.0 226.1 jit_solution(17618791465777065073)
XLA Ops:
  0.0 219.2 %sums.1 = bf16[4,768,3072]{2,1,0:T(8,128)(2,1)S(1)} custom-call(bf16[4,4096,768]{2,1,0:T(8,128)(2,1)} %bitcast.2, bf16[4,4096,3072]{2,1,0:T(8,128)(2,1)} %bitcast.1.g_hbm), custom_call_target="tpu_custom_call" | custom-call | tf_op jit(solution)/shard_map/sums/pallas_call | solution.py:147
  219.2 6.9 %copy.4 = bf16[4,768,3072]{2,1,0:T(8,128)(2,1)} copy(bf16[4,768,3072]{2,1,0:T(8,128)(2,1)S(1)} %sums.1) | data formatting | bytes 37748736

commit v2 on v0

v2 whole, which is shorter than its diff:
```python
import jax
import jax.numpy as jnp
from jax import lax
from jax.experimental import pallas as pl
from jax.experimental.pallas import tpu as pltpu
from jax.sharding import PartitionSpec as P

MESH = pl.DeviceIdType.MESH
WIDTH = 512
PART = 128
FIRST = ((0, 128), (128, 256))


def kernel(a_hbm, g_hbm, out, a_buf, g_buf, own, stage, first_stage, came,
           a_first, a_sem, g_sem, d_send, first_send, d_recv,
           x_send, x_recv, f_send, f_recv):
    mats, tokens, rows = a_hbm.shape
    cols = g_hbm.shape[2]
    half = rows // 2
    tiles = cols // WIDTH
    steps = mats * tiles
    parts = half // PART
    f32, bf16 = jnp.float32, jnp.bfloat16

    rep = lax.axis_index("rep")
    me = lax.axis_index("dp")
    core = lax.rem(me, 2)
    partner = me + 1 - 2 * core
    across = lax.rem(me + 2, 4)

    def span(start, size, unit):
        return pl.ds(pl.multiple_of(start, unit), size)

    def block(which, n, r0, nr, c0, nc):
        return out.at[n, span(which * half + r0, nr, 64), span(c0, nc, 256)]

    def remote(src, dst, send, recv, to):
        return pltpu.make_async_remote_copy(
            src, dst, send, recv, device_id=(rep, to), device_id_type=MESH)

    def d_copy(src, send, recv, *at):
        return remote(src, block(1 - core, *at), send, recv, partner)

    def d_arrival(src, send, recv, *at):
        return remote(src, block(core, *at), send, recv, partner)

    def x_copy(j, n, r0, nr, c0, nc):
        return remote(block(core, n, r0, nr, c0, nc),
                      came.at[n, span(r0, nr, 64), span(c0, nc, 256)],
                      x_send.at[j], x_recv.at[j], across)

    def f_copy(j, *at):
        return remote(block(core, *at), block(core, *at), f_send.at[j], f_recv.at[j], partner)

    def f_arrival(j, *at):
        return remote(block(1 - core, *at), block(1 - core, *at), f_send.at[j], f_recv.at[j], partner)

    def a_copy(n):
        return pltpu.make_async_copy(a_hbm.at[n], a_buf.at[lax.rem(n, 2)], a_sem.at[lax.rem(n, 2)])

    def g_copy(i):
        return pltpu.make_async_copy(
            g_hbm.at[i // tiles, :, span(lax.rem(i, tiles) * WIDTH, WIDTH, WIDTH)],
            g_buf.at[lax.rem(i, 2)], g_sem.at[lax.rem(i, 2)])

    def term(which, slot, g, r0, nr):
        return lax.dot_general(
            a_buf[slot, :, span(which * half + r0, nr, 128)], g,
            (((0,), (0,)), ((), ())), preferred_element_type=f32)

    def add_term(b, value):
        b[...] = (value + b[...].astype(f32)).astype(bf16)

    def first_a(which, k):
        r0, nr = FIRST[k]
        at = span(which * half + r0, nr, 128)
        return pltpu.make_async_copy(
            a_hbm.at[0, :, at], a_buf.at[0, :, at], a_first.at[k, which])

    first_a(0, 0).start()
    first_a(1, 0).start()
    g_copy(0).start()
    first_a(0, 1).start()
    first_a(1, 1).start()
    g_copy(1).start()
    a_copy(1).start()

    barrier = pltpu.get_barrier_semaphore()
    for other in (partner, across):
        pl.semaphore_signal(barrier, 1, device_id=(rep, other), device_id_type=MESH)

    for k, (r0, nr) in enumerate(FIRST):
        first_a(0, k).wait()
        first_a(1, k).wait()
        if k == 0:
            g_copy(0).wait()
        at = (0, r0, nr, 0, WIDTH)
        g = g_buf.at[0]
        held = first_stage.at[k, pl.ds(0, nr)]
        held[...] = term(1 - core, 0, g[...], r0, nr).astype(bf16)
        if k == 0:
            pl.semaphore_wait(barrier, 2)
        d_copy(held, first_send.at[k], d_recv.at[k], *at).start()
        own[pl.ds(0, nr)] = term(core, 0, g[...], r0, nr)
        d_arrival(held, first_send.at[k], d_recv.at[k], *at).wait_recv()
        add_term(block(core, *at), own[pl.ds(0, nr)])
        x_copy(k, *at).start()

    def place(i):
        return i // tiles, lax.rem(i, tiles) * WIDTH

    def number(i, r):
        return len(FIRST) + (i - 1) * parts + r

    def tile_d(i):
        n, c0 = place(i)
        slot = lax.rem(i, 2)
        return stage.at[slot], d_send.at[slot], d_recv.at[len(FIRST) - 1 + i], n, 0, half, c0, WIDTH

    @pl.loop(1, steps)
    def _(i):
        n, c0 = place(i)
        slot = lax.rem(i, 2)

        @pl.when(i + 1 < steps)
        def _():
            g_copy(i + 1).start()

        @pl.when(c0 == 0)
        def _():
            a_copy(n).wait()

        @pl.when((c0 == 0) & (n + 1 < mats))
        def _():
            a_copy(n + 1).start()

        g_copy(i).wait()

        @pl.when(i >= 3)
        def _():
            d_copy(*tile_d(i - 2)).wait_send()

        stage[slot] = term(1 - core, lax.rem(n, 2), g_buf[slot], 0, half).astype(bf16)
        d_copy(*tile_d(i)).start()
        own[...] = term(core, lax.rem(n, 2), g_buf[slot], 0, half)
        d_arrival(*tile_d(i)).wait_recv()
        for r in range(parts):
            at = (n, r * PART, PART, c0, WIDTH)
            add_term(block(core, *at), own[pl.ds(r * PART, PART)])
            x_copy(number(i, r), *at).start()

    for k, (r0, nr) in enumerate(FIRST):
        d_copy(first_stage.at[k, pl.ds(0, nr)], first_send.at[k], d_recv.at[k],
               0, r0, nr, 0, WIDTH).wait_send()
    for i in (steps - 2, steps - 1):
        d_copy(*tile_d(i)).wait_send()

    def finish(j, n, r0, nr, c0, nc):
        at = (n, r0, nr, c0, nc)
        x_copy(j, *at).wait()
        add_term(block(core, *at), came[n, span(r0, nr, 64), span(c0, nc, 256)].astype(f32))
        f_copy(j, *at).start()

    for k, at in enumerate(FIRST):
        finish(k, 0, *at, 0, WIDTH)

    @pl.loop(1, steps)
    def _(i):
        n, c0 = place(i)
        for r in range(parts):
            finish(number(i, r), n, r * PART, PART, c0, WIDTH)

    for k, at in enumerate(FIRST):
        f_copy(k, 0, *at, 0, WIDTH).wait_send()
        f_arrival(k, 0, *at, 0, WIDTH).wait_recv()

    @pl.loop(1, steps)
    def _(i):
        n, c0 = place(i)
        for r in range(parts):
            at = (n, r * PART, PART, c0, WIDTH)
            f_copy(number(i, r), *at).wait_send()
            f_arrival(number(i, r), *at).wait_recv()


def solution(mesh):
    def step(a, g):
        a, g = a[0], g[0]
        mats, tokens, rows = a.shape
        cols = g.shape[2]
        half = rows // 2
        steps = mats * (cols // WIDTH)
        copies = len(FIRST) + (steps - 1) * (half // PART)
        dma = pltpu.SemaphoreType.DMA
        return pl.pallas_call(
            kernel,
            out_shape=pltpu.VMEM((mats, rows, cols), jnp.bfloat16),
            in_specs=[pl.BlockSpec(memory_space=pl.ANY)] * 2,
            out_specs=pl.BlockSpec(memory_space=pltpu.VMEM),
            scratch_shapes=[
                pltpu.VMEM((2, tokens, rows), jnp.bfloat16),
                pltpu.VMEM((2, tokens, WIDTH), jnp.bfloat16),
                pltpu.VMEM((half, WIDTH), jnp.float32),
                pltpu.VMEM((2, half, WIDTH), jnp.bfloat16),
                pltpu.VMEM((len(FIRST), half, WIDTH), jnp.bfloat16),
                pltpu.VMEM((mats, half, cols), jnp.bfloat16),
                dma((2, 2)), dma((2,)), dma((2,)), dma((2,)), dma((len(FIRST),)),
                dma((len(FIRST) + steps - 1,)),
                dma((copies,)), dma((copies,)), dma((copies,)), dma((copies,)),
            ],
            compiler_params=pltpu.CompilerParams(
                collective_id=0, has_side_effects=True, vmem_limit_bytes=42 << 20),
            name="sums",
        )(a, g)

    return jax.shard_map(
        step, mesh=mesh, in_specs=(P(("rep", "dp")), P(("rep", "dp"))), out_specs=P("rep"),
        check_vma=False)
```

time: 730 us -> 223 us (0.31)
  blocking collectives: 641 us -> 0 us
  Pallas kernels: 0 us -> 216 us
  matrix products: 88.8 us -> 0 us
    dot_general x1 -> x0, blocking collectives: 641 us -> none  [step(): jnp.einsum('rsntd,rsntf->rndf', a, g, preferred_element_type=jnp.float32)]
    pallas_call x0 -> x1, Pallas kernels: none -> 216 us  [step(): pl.pallas_call(kernel, out_shape=pltpu.VMEM((mats, rows, cols), jnp.bfloa...]
    dot_general x1 -> x0, matrix products: 88.8 us -> none  [step(): jnp.einsum('rsntd,rsntf->rndf', a, g, preferred_element_type=jnp.float32)]
where the time goes in v2:
time: 223 us
  Pallas kernels  216 us (97%)
  local copies, waits for them, and re-layouts  6.85 us (3%)
    pallas_call x1, Pallas kernels, step(): pl.pallas_call(kernel, out_shape=pltpu.VMEM((mats, rows, cols), jnp.bfloa...  216 us
    unnamed x1, local copies, waits for them, and re-layouts  6.85 us

profile of v2, /device:TPU:0, one launch (start us, length us, event | category | flops | bytes accessed | tf_op | source)
XLA Modules:
  0.0 222.8 jit_solution(10345390046052781590)
XLA Ops:
  0.0 216.0 %sums.1 = bf16[4,768,3072]{2,1,0:T(8,128)(2,1)S(1)} custom-call(bf16[4,4096,768]{2,1,0:T(8,128)(2,1)} %bitcast.2, bf16[4,4096,3072]{2,1,0:T(8,128)(2,1)} %bitcast.1.g_hbm), custom_call_target="tpu_custom_call" | custom-call | tf_op jit(solution)/shard_map/sums/pallas_call | solution.py:195
  216.0 6.9 %copy.4 = bf16[4,768,3072]{2,1,0:T(8,128)(2,1)} copy(bf16[4,768,3072]{2,1,0:T(8,128)(2,1)S(1)} %sums.1) | data formatting | bytes 37748736
